TPU v7x, 32 devices: a whole 2x2x4 slice. The times are simulated.
32 devices in a mesh: row: 2 (over x), col: 16 (over z, y, core).
Axes of the slice: x: 2, y: 2, z: 4, core: 2. Of those that a mesh axis runs over, the one named last changes fastest.
Arguments:
- eigvecs: float32 [16384, 4096], P('row', 'col'), may hold values from -6 to 6
- v_panels: float32 [8, 16384, 256], P(None, 'row', 'col'), as said below
- t_panels: float32 [8, 256, 256], P(None, None, 'col'), as said below
Outputs:
- rotated: float32 [16384, 4096], P('row', 'col')
Inputs may be any that keep to these rules, and one draw needn't show every extreme that they name: `v_panels`: in panel k, vector j is zero in rows above k * 256 + j + 1, equals 1 in that row and is dense below it. t_panels[k] is upper triangular and V_k t_panels[k] V_k^T = I minus the product of the panel's 256 Householder reflections, each I - 2 v v^T / (v^T v), taken in the order of j; its diagonal lies in (0, 2].
All inputs are finite; a program needn't handle non-finite values.
Results may differ from a plain program's by a relative error of at most 0.00015.
Values sent between devices are 32-bit elements; how exact they have to be, the bound alone decides.
A program may use at most 192 MiB of HBM per device.

v0:
```python
import jax
import jax.numpy as jnp
from jax import lax
from jax.sharding import PartitionSpec as P

exact_precision = lax.Precision.HIGHEST


def matmul(left, right):
    return jnp.dot(left, right, preferred_element_type=jnp.float32, precision=exact_precision)


def project(left, right):
    return lax.dot_general(
        left,
        right,
        (((0,), (0,)), ((), ())),
        precision=exact_precision,
        preferred_element_type=jnp.float32,
    )


def local(eigvecs, v_panels, t_panels):
    panels_total = v_panels.shape[0]
    every_v, every_t = (
        lax.all_gather(v_panels, "col", axis=2, tiled=True),
        lax.all_gather(t_panels, "col", axis=2, tiled=True),
    )
    current = eigvecs
    for panel_index in reversed(range(panels_total)):
        vectors = every_v[panel_index]
        factor = every_t[panel_index]
        projected = lax.psum(project(vectors, current), "row")
        current = current - matmul(vectors, matmul(factor, projected))
    return current


def solution(mesh):
    in_specs = (P("row", "col"), P(None, "row", "col"), P(None, None, "col"))
    out_specs = P("row", "col")
    return jax.shard_map(local, mesh=mesh, in_specs=in_specs, out_specs=out_specs, check_vma=False)
```

profile of v0, /device:TPU:0, one launch (start us, length us, event | category | flops | bytes accessed | tf_op | source)
XLA Modules:
  0.0 791.7 jit_solution(15002217065631639125)
XLA Ops:
  8.1 329.7 %all-gather.3.cloned.1.call-done = f32[8,8192,256]{1,2,0:T(8,128)} async-done(((f32[8,8192,16]{1,2,0:T(8,128)}), f32[8,8192,256]{1,2,0:T(8,128)}) %all-gather.3.cloned.1.call-update) | async-done | bytes 67108880 | tf_op jit(solution)/shard_map/all_gather | solution.py:26
  337.7 11.4 %fusion.8 = f32[256,256]{1,0:T(8,128)} fusion(f32[8192,256]{1,0:T(8,128)} %param.3, f32[8,8192,256]{1,2,0:T(8,128)} %all-gather.3.cloned.1.call-done), kind=kOutput, calls=%fused_computation.24 | convolution fusion | flops 6442450944 | bytes 17039360 | tf_op jit(solution)/shard_map/dot_general | solution.py:14
  349.5 8.9 %copy.4 = f32[8192,256]{0,1:T(8,128)} copy(f32[8192,256]{1,0:T(8,128)} %param.3) | data formatting | bytes 16777216 | tf_op args[0]
  358.4 23.0 %all-gather.5.cloned.1.call-done = f32[8,256,256]{1,2,0:T(8,128)} async-done(((f32[8,256,16]{1,2,0:T(8,128)}), f32[8,256,256]{1,2,0:T(8,128)}) %all-gather.5.cloned.1.call-update) | async-done | bytes 2097168 | tf_op jit(solution)/shard_map/all_gather | solution.py:27
  381.4 24.3 %all-reduce.9.cloned.1.call-done = f32[256,256]{1,0:T(8,128)} async-done(((f32[256,256]{1,0:T(8,128)}), f32[256,256]{1,0:T(8,128)}) %all-reduce.9.cloned.1.call-update) | async-done | bytes 262160 | tf_op jit(solution)/shard_map/psum | solution.py:33
  407.4 11.9 %fusion.7 = f32[8192,256]{0,1:T(8,128)S(1)} fusion(f32[8192,256]{0,1:T(8,128)} %copy.4, f32[256,256]{1,0:T(8,128)S(1)} %fusion.30, f32[8,8192,256]{1,2,0:T(8,128)} %all-gather.3.cloned.1.call-done), kind=kOutput, calls=%fused_computation.15 | convolution fusion | flops 6444548096 | bytes 25427968 | tf_op jit(solution)/shard_map/dot_general | solution.py:10
  419.3 3.4 copy-done
  422.7 10.3 %fusion.22 = f32[256,256]{0,1:T(8,128)} fusion(f32[8192,256]{0,1:T(8,128)S(1)} %fusion.7, f32[8,8192,256]{1,2,0:T(8,128)} %all-gather.3.cloned.1.call-done), kind=kOutput, calls=%fused_computation.38 | convolution fusion | flops 6442450944 | bytes 17039360 | tf_op jit(solution)/shard_map/dot_general | solution.py:14
  433.3 23.1 %all-reduce.11.cloned.1.call-done = f32[256,256]{0,1:T(8,128)} async-done(((f32[256,256]{0,1:T(8,128)}), f32[256,256]{0,1:T(8,128)}) %all-reduce.11.cloned.1.call-update) | async-done | bytes 262160 | tf_op jit(solution)/shard_map/psum | solution.py:33
  457.8 11.9 %fusion.6 = f32[8192,256]{0,1:T(8,128)S(1)} fusion(f32[8192,256]{0,1:T(8,128)} %copy-done, f32[256,256]{1,0:T(8,128)S(1)} %fusion.29, f32[8,8192,256]{1,2,0:T(8,128)} %all-gather.3.cloned.1.call-done), kind=kOutput, calls=%fused_computation.13 | convolution fusion | flops 6444548096 | bytes 25427968 | tf_op jit(solution)/shard_map/dot_general | solution.py:10
  469.7 3.4 copy-done.1
  473.1 10.1 %fusion.21 = f32[256,256]{0,1:T(8,128)} fusion(f32[8192,256]{0,1:T(8,128)S(1)} %fusion.6, f32[8,8192,256]{1,2,0:T(8,128)} %all-gather.3.cloned.1.call-done), kind=kOutput, calls=%fused_computation.37 | convolution fusion | flops 6442450944 | bytes 17039360 | tf_op jit(solution)/shard_map/dot_general | solution.py:14
  483.9 22.8 %all-reduce.13.cloned.1.call-done = f32[256,256]{0,1:T(8,128)} async-done(((f32[256,256]{0,1:T(8,128)}), f32[256,256]{0,1:T(8,128)}) %all-reduce.13.cloned.1.call-update) | async-done | bytes 262160 | tf_op jit(solution)/shard_map/psum | solution.py:33
  508.0 11.9 %fusion.5 = f32[8192,256]{0,1:T(8,128)S(1)} fusion(f32[8192,256]{0,1:T(8,128)} %copy-done.1, f32[256,256]{1,0:T(8,128)S(1)} %fusion.28, f32[8,8192,256]{1,2,0:T(8,128)} %all-gather.3.cloned.1.call-done), kind=kOutput, calls=%fused_computation.11 | convolution fusion | flops 6444548096 | bytes 25427968 | tf_op jit(solution)/shard_map/dot_general | solution.py:10
  519.9 3.4 copy-done.2
  523.3 10.1 %fusion.20 = f32[256,256]{0,1:T(8,128)} fusion(f32[8192,256]{0,1:T(8,128)S(1)} %fusion.5, f32[8,8192,256]{1,2,0:T(8,128)} %all-gather.3.cloned.1.call-done), kind=kOutput, calls=%fused_computation.36 | convolution fusion | flops 6442450944 | bytes 17039360 | tf_op jit(solution)/shard_map/dot_general | solution.py:14
  533.7 23.2 %all-reduce.15.cloned.1.call-done = f32[256,256]{0,1:T(8,128)} async-done(((f32[256,256]{0,1:T(8,128)}), f32[256,256]{0,1:T(8,128)}) %all-reduce.15.cloned.1.call-update) | async-done | bytes 262160 | tf_op jit(solution)/shard_map/psum | solution.py:33
  558.3 11.9 %fusion.4 = f32[8192,256]{0,1:T(8,128)S(1)} fusion(f32[8192,256]{0,1:T(8,128)} %copy-done.2, f32[256,256]{1,0:T(8,128)S(1)} %fusion.27, f32[8,8192,256]{1,2,0:T(8,128)} %all-gather.3.cloned.1.call-done), kind=kOutput, calls=%fused_computation.9 | convolution fusion | flops 6444548096 | bytes 25427968 | tf_op jit(solution)/shard_map/dot_general | solution.py:10
  570.2 3.4 copy-done.3
  573.6 10.1 %fusion.19 = f32[256,256]{0,1:T(8,128)} fusion(f32[8192,256]{0,1:T(8,128)S(1)} %fusion.4, f32[8,8192,256]{1,2,0:T(8,128)} %all-gather.3.cloned.1.call-done), kind=kOutput, calls=%fused_computation.35 | convolution fusion | flops 6442450944 | bytes 17039360 | tf_op jit(solution)/shard_map/dot_general | solution.py:14
  584.0 23.2 %all-reduce.17.cloned.1.call-done = f32[256,256]{0,1:T(8,128)} async-done(((f32[256,256]{0,1:T(8,128)}), f32[256,256]{0,1:T(8,128)}) %all-reduce.17.cloned.1.call-update) | async-done | bytes 262160 | tf_op jit(solution)/shard_map/psum | solution.py:33
  608.5 11.9 %fusion.3 = f32[8192,256]{0,1:T(8,128)S(1)} fusion(f32[8192,256]{0,1:T(8,128)} %copy-done.3, f32[256,256]{1,0:T(8,128)S(1)} %fusion.26, f32[8,8192,256]{1,2,0:T(8,128)} %all-gather.3.cloned.1.call-done), kind=kOutput, calls=%fused_computation.7 | convolution fusion | flops 6444548096 | bytes 25427968 | tf_op jit(solution)/shard_map/dot_general | solution.py:10
  623.8 10.1 %fusion.18 = f32[256,256]{0,1:T(8,128)} fusion(f32[8192,256]{0,1:T(8,128)S(1)} %fusion.3, f32[8,8192,256]{1,2,0:T(8,128)} %all-gather.3.cloned.1.call-done), kind=kOutput, calls=%fused_computation.34 | convolution fusion | flops 6442450944 | bytes 17039360 | tf_op jit(solution)/shard_map/dot_general | solution.py:14
  634.3 23.2 %all-reduce.19.cloned.1.call-done = f32[256,256]{0,1:T(8,128)} async-done(((f32[256,256]{0,1:T(8,128)}), f32[256,256]{0,1:T(8,128)}) %all-reduce.19.cloned.1.call-update) | async-done | bytes 262160 | tf_op jit(solution)/shard_map/psum | solution.py:33
  658.8 11.9 %fusion.2 = f32[8192,256]{0,1:T(8,128)S(1)} fusion(f32[8192,256]{0,1:T(8,128)} %copy-done.4, f32[256,256]{1,0:T(8,128)S(1)} %fusion.25, f32[8,8192,256]{1,2,0:T(8,128)} %all-gather.3.cloned.1.call-done), kind=kOutput, calls=%fused_computation.5 | convolution fusion | flops 6444548096 | bytes 25427968 | tf_op jit(solution)/shard_map/dot_general | solution.py:10
  674.1 10.1 %fusion.17 = f32[256,256]{0,1:T(8,128)} fusion(f32[8192,256]{0,1:T(8,128)S(1)} %fusion.2, f32[8,8192,256]{1,2,0:T(8,128)} %all-gather.3.cloned.1.call-done), kind=kOutput, calls=%fused_computation.33 | convolution fusion | flops 6442450944 | bytes 17039360 | tf_op jit(solution)/shard_map/dot_general | solution.py:14
  684.7 22.9 %all-reduce.21.cloned.1.call-done = f32[256,256]{0,1:T(8,128)} async-done(((f32[256,256]{0,1:T(8,128)}), f32[256,256]{0,1:T(8,128)}) %all-reduce.21.cloned.1.call-update) | async-done | bytes 262160 | tf_op jit(solution)/shard_map/psum | solution.py:33
  709.0 11.9 %fusion.1 = f32[8192,256]{0,1:T(8,128)S(1)} fusion(f32[8192,256]{0,1:T(8,128)} %copy-done.5, f32[256,256]{1,0:T(8,128)S(1)} %fusion.24, f32[8,8192,256]{1,2,0:T(8,128)} %all-gather.3.cloned.1.call-done), kind=kOutput, calls=%fused_computation.3 | convolution fusion | flops 6444548096 | bytes 25427968 | tf_op jit(solution)/shard_map/dot_general | solution.py:10
  724.3 10.1 %fusion.16 = f32[256,256]{0,1:T(8,128)} fusion(f32[8192,256]{0,1:T(8,128)S(1)} %fusion.1, f32[8,8192,256]{1,2,0:T(8,128)} %all-gather.3.cloned.1.call-done), kind=kOutput, calls=%fused_computation.32 | convolution fusion | flops 6442450944 | bytes 17039360 | tf_op jit(solution)/shard_map/dot_general | solution.py:14
  734.5 23.5 %all-reduce.23.cloned.1.call-done = f32[256,256]{0,1:T(8,128)} async-done(((f32[256,256]{0,1:T(8,128)}), f32[256,256]{0,1:T(8,128)}) %all-reduce.23.cloned.1.call-update) | async-done | bytes 262160 | tf_op jit(solution)/shard_map/psum | solution.py:33
  759.3 16.4 %fusion = f32[8192,256]{0,1:T(8,128)} fusion(f32[8192,256]{0,1:T(8,128)} %copy-done.6, f32[256,256]{1,0:T(8,128)S(1)} %fusion.23, f32[8,8192,256]{1,2,0:T(8,128)} %all-gather.3.cloned.1.call-done), kind=kOutput, calls=%fused_computation.1 | convolution fusion | flops 6444548096 | bytes 25427968 | tf_op jit(solution)/shard_map/dot_general | solution.py:10
  775.7 9.0 %copy.5 = f32[8192,256]{1,0:T(8,128)} copy(f32[8192,256]{0,1:T(8,128)} %fusion) | data formatting | bytes 16777216 | tf_op jit(solution)/shard_map/sub | solution.py:34
  (40 shorter events, 25.3 us)
Async XLA Ops:
  6.5 331.2 %all-gather.3.cloned.1.call-start = ((), (), s32[]{:S(2)}) async-start(), calls=%async_computation | async-start | bytes 71303168 | tf_op jit(solution)/shard_map/all_gather | solution.py:26
  7.3 374.2 %all-gather.5.cloned.1.call-start = ((), (), s32[]{:S(2)}) async-start(), calls=%async_computation.2 | async-start | bytes 2228224 | tf_op jit(solution)/shard_map/all_gather | solution.py:27
  8.0 397.7 %all-reduce.9.cloned.1.call-start = ((), (), s32[]{:S(2)}) async-start(), calls=%async_computation.1 | async-start | bytes 524288 | tf_op jit(solution)/shard_map/psum | solution.py:33
  349.1 107.3 %all-reduce.11.cloned.1.call-start = ((), (), s32[]{:S(2)}) async-start(), calls=%async_computation.3 | async-start | bytes 524288 | tf_op jit(solution)/shard_map/psum | solution.py:33
  419.3 3.4 copy-start
  422.7 33.8 %copy-start.7 = (f32[8,256,256]{1,2,0:T(8,128)S(1)}, f32[8,256,256]{1,2,0:T(8,128)}, u32[]{:S(2)}) copy-start(f32[8,256,256]{1,2,0:T(8,128)} %all-gather.5.cloned.1.call-done) | copy-start | bytes 6291460
  433.0 73.7 %all-reduce.13.cloned.1.call-start = ((), (), s32[]{:S(2)}) async-start(), calls=%async_computation.4 | async-start | bytes 524288 | tf_op jit(solution)/shard_map/psum | solution.py:33
  469.7 3.4 copy-start.1
  483.2 73.7 %all-reduce.15.cloned.1.call-start = ((), (), s32[]{:S(2)}) async-start(), calls=%async_computation.5 | async-start | bytes 524288 | tf_op jit(solution)/shard_map/psum | solution.py:33
  519.9 3.4 copy-start.2
  533.5 73.7 %all-reduce.17.cloned.1.call-start = ((), (), s32[]{:S(2)}) async-start(), calls=%async_computation.6 | async-start | bytes 524288 | tf_op jit(solution)/shard_map/psum | solution.py:33
  570.2 3.4 copy-start.3
  583.7 73.7 %all-reduce.19.cloned.1.call-start = ((), (), s32[]{:S(2)}) async-start(), calls=%async_computation.7 | async-start | bytes 524288 | tf_op jit(solution)/shard_map/psum | solution.py:33
  620.4 3.4 copy-start.4
  634.0 73.7 %all-reduce.21.cloned.1.call-start = ((), (), s32[]{:S(2)}) async-start(), calls=%async_computation.8 | async-start | bytes 524288 | tf_op jit(solution)/shard_map/psum | solution.py:33
  670.7 3.4 copy-start.5
  684.2 73.7 %all-reduce.23.cloned.1.call-start = ((), (), s32[]{:S(2)}) async-start(), calls=%async_computation.9 | async-start | bytes 524288 | tf_op jit(solution)/shard_map/psum | solution.py:33
  720.9 3.4 copy-start.6
Sparse Core Ops, SparseCore 0:
  8.9 328.7 all-gather.2
  339.9 41.4 all-gather.4
  383.7 22.0 all-reduce.8
  433.1 23.2 all-reduce.10
  483.3 23.2 all-reduce.12
  533.6 23.2 all-reduce.14
  583.8 23.2 all-reduce.16
  634.1 23.2 all-reduce.18
  684.3 23.2 all-reduce.20
  734.6 23.2 all-reduce.22
where the time goes:
time: 796 us; the launch traced here: 792 us
  waiting for transfers between devices  540 us (68%)
  matrix products  193 us (24%)
  local copies, waits for them, and re-layouts  41.6 us (5%)
  between operations  13.9 us (2%)
    all_gather x1, waiting for transfers between devices, local(): lax.all_gather(v_panels, 'col', axis=2, tiled=True)  330 us
    psum x8, waiting for transfers between devices, local(): projected = lax.psum(project(vectors, current), 'row')  186 us
    dot_general x16, matrix products, matmul(): jnp.dot(left, right, preferred_element_type=jnp.float32, precision=exact_...  111 us
    dot_general x8, matrix products, project(): lax.dot_general(left, right, (((0,), (0,)), ((), ())), precision=exact_pr...  82.4 us
    unnamed x17, local copies, waits for them, and re-layouts  32.7 us
    all_gather x1, waiting for transfers between devices, local(): lax.all_gather(t_panels, 'col', axis=2, tiled=True)  23 us
  transfers between devices with their start and end apart: 10, of which 10 were waited for; matrix products, arithmetic and copies ran while one was open for 3% of the time, Pallas kernels for 0%

commit v1 on v0

--- a/solution.py
+++ b/solution.py
@@ -30,7 +30,7 @@
     for panel_index in reversed(range(panels_total)):
         vectors = every_v[panel_index]
         factor = every_t[panel_index]
-        projected = lax.psum(project(vectors, current), "row")
+        projected = jnp.sum(lax.all_gather(project(vectors, current), "row"), axis=0)
         current = current - matmul(vectors, matmul(factor, projected))
     return current
 

time: 796 us -> 661 us (0.83)
  waiting for transfers between devices: 540 us -> 345 us
  blocking collectives: 0 us -> 64.3 us
  local copies, waits for them, and re-layouts: 41.6 us -> 20.3 us
  matrix products: 193 us -> 208 us
    psum x8 -> x0, waiting for transfers between devices: 186 us -> none  [local(): projected = lax.psum(project(vectors, current), 'row')]
    all_gather x0 -> x8, blocking collectives: none -> 64.3 us  [local(): lax.all_gather(project(vectors, current), 'row')]
    unnamed x17 -> x15, local copies, waits for them, and re-layouts: 32.7 us -> 8.95 us
    dot_general x8, matrix products: 82.4 us -> 98 us  [project(): lax.dot_general(left, right, (((0,), (0,)), ((), ())), precision=exact_pr...]
    all_gather x1, waiting for transfers between devices: 330 us -> 321 us  [local(): lax.all_gather(v_panels, 'col', axis=2, tiled=True)]
  transfers between devices with their start and end apart: 10 -> 2, of which waited for: 10 -> 2; matrix products, arithmetic and copies ran while one was open for 3% -> 3% of each run, Pallas kernels for 0% -> 0%
where the time goes in v1:
time: 661 us; the launch traced here: 657 us
  waiting for transfers between devices  345 us (52%)
  matrix products  208 us (31%)
  blocking collectives  64.3 us (10%)
  local copies, waits for them, and re-layouts  20.3 us (3%)
  between operations  14.3 us (2%)
    all_gather x1, waiting for transfers between devices, local(): lax.all_gather(v_panels, 'col', axis=2, tiled=True)  321 us
    dot_general x16, matrix products, matmul(): jnp.dot(left, right, preferred_element_type=jnp.float32, precision=exact_...  110 us
    dot_general x8, matrix products, project(): lax.dot_general(left, right, (((0,), (0,)), ((), ())), precision=exact_pr...  98 us
    all_gather x8, blocking collectives, local(): lax.all_gather(project(vectors, current), 'row')  64.3 us
    all_gather x1, waiting for transfers between devices, local(): lax.all_gather(t_panels, 'col', axis=2, tiled=True)  23.3 us
  transfers between devices with their start and end apart: 2, of which 2 were waited for; matrix products, arithmetic and copies ran while one was open for 3% of the time, Pallas kernels for 0%

profile of v1, /device:TPU:0, one launch (start us, length us, event | category | flops | bytes accessed | tf_op | source)
XLA Modules:
  0.0 657.1 jit_solution(12147726348671748409)
XLA Ops:
  8.0 8.9 %copy.6 = f32[8192,256]{0,1:T(8,128)} copy(f32[8192,256]{1,0:T(8,128)} %param.3) | data formatting | bytes 16777216 | tf_op args[0]
  16.9 320.8 %all-gather.11.cloned.1.call-done = f32[8,8192,256]{1,2,0:T(8,128)} async-done(((f32[8,8192,16]{1,2,0:T(8,128)}), f32[8,8192,256]{1,2,0:T(8,128)}) %all-gather.11.cloned.1.call-update) | async-done | bytes 67108880 | tf_op jit(solution)/shard_map/all_gather | solution.py:26
  337.7 10.7 %fusion.8 = f32[256,256]{1,0:T(8,128)S(1)} fusion(f32[8192,256]{1,0:T(8,128)} %param.3, f32[8,8192,256]{1,2,0:T(8,128)} %all-gather.11.cloned.1.call-done), kind=kOutput, calls=%fused_computation.24 | convolution fusion | flops 6442450944 | bytes 17039360 | tf_op jit(solution)/shard_map/dot_general | solution.py:14
  348.4 9.6 %all-gather = f32[512,256]{1,0:T(8,128)S(1)} all-gather(f32[256,256]{1,0:T(8,128)S(1)} %fusion.8), channel_id=2, replica_groups=mesh['row'=2,'col'=16] {'row'}, dimensions={0}, use_global_device_ids=true | all-gather | bytes 786432 | tf_op jit(solution)/shard_map/all_gather | solution.py:33
  358.1 23.3 %all-gather.13.cloned.1.call-done = f32[8,256,256]{1,2,0:T(8,128)} async-done(((f32[8,256,16]{1,2,0:T(8,128)}), f32[8,256,256]{1,2,0:T(8,128)}) %all-gather.13.cloned.1.call-update) | async-done | bytes 2097168 | tf_op jit(solution)/shard_map/all_gather | solution.py:27
  381.4 1.5 fusion.30
  383.0 11.9 %fusion.7 = f32[8192,256]{0,1:T(8,128)S(1)} fusion(f32[8192,256]{0,1:T(8,128)} %copy.6, f32[256,256]{1,0:T(8,128)S(1)} %fusion.30, f32[8,8192,256]{1,2,0:T(8,128)} %all-gather.11.cloned.1.call-done), kind=kOutput, calls=%fused_computation.15 | convolution fusion | flops 6444548096 | bytes 25427968 | tf_op jit(solution)/shard_map/dot_general | solution.py:10
  394.9 12.5 %fusion.22 = f32[256,256]{0,1:T(8,128)S(1)} fusion(f32[8192,256]{0,1:T(8,128)S(1)} %fusion.7, f32[8,8192,256]{1,2,0:T(8,128)} %all-gather.11.cloned.1.call-done), kind=kOutput, calls=%fused_computation.38 | convolution fusion | flops 6442450944 | bytes 17039360 | tf_op jit(solution)/shard_map/dot_general | solution.py:14
  407.4 9.3 %all-gather.1 = f32[512,256]{0,1:T(8,128)S(1)} all-gather(f32[256,256]{0,1:T(8,128)S(1)} %fusion.22), channel_id=3, replica_groups=mesh['row'=2,'col'=16] {'row'}, dimensions={0}, use_global_device_ids=true | all-gather | bytes 786432 | tf_op jit(solution)/shard_map/all_gather | solution.py:33
  418.9 11.9 %fusion.6 = f32[8192,256]{0,1:T(8,128)S(1)} fusion(f32[8192,256]{0,1:T(8,128)} %copy-done.1, f32[256,256]{1,0:T(8,128)S(1)} %fusion.29, f32[8,8192,256]{1,2,0:T(8,128)} %all-gather.11.cloned.1.call-done), kind=kOutput, calls=%fused_computation.13 | convolution fusion | flops 6444548096 | bytes 25427968 | tf_op jit(solution)/shard_map/dot_general | solution.py:10
  430.9 12.5 %fusion.21 = f32[256,256]{0,1:T(8,128)S(1)} fusion(f32[8192,256]{0,1:T(8,128)S(1)} %fusion.6, f32[8,8192,256]{1,2,0:T(8,128)} %all-gather.11.cloned.1.call-done), kind=kOutput, calls=%fused_computation.37 | convolution fusion | flops 6442450944 | bytes 17039360 | tf_op jit(solution)/shard_map/dot_general | solution.py:14
  443.3 8.5 %all-gather.2 = f32[512,256]{0,1:T(8,128)S(1)} all-gather(f32[256,256]{0,1:T(8,128)S(1)} %fusion.21), channel_id=4, replica_groups=mesh['row'=2,'col'=16] {'row'}, dimensions={0}, use_global_device_ids=true | all-gather | bytes 786432 | tf_op jit(solution)/shard_map/all_gather | solution.py:33
  454.1 11.9 %fusion.5 = f32[8192,256]{0,1:T(8,128)S(1)} fusion(f32[8192,256]{0,1:T(8,128)} %copy-done.2, f32[256,256]{1,0:T(8,128)S(1)} %fusion.28, f32[8,8192,256]{1,2,0:T(8,128)} %all-gather.11.cloned.1.call-done), kind=kOutput, calls=%fused_computation.11 | convolution fusion | flops 6444548096 | bytes 25427968 | tf_op jit(solution)/shard_map/dot_general | solution.py:10
  466.0 12.5 %fusion.20 = f32[256,256]{0,1:T(8,128)S(1)} fusion(f32[8192,256]{0,1:T(8,128)S(1)} %fusion.5, f32[8,8192,256]{1,2,0:T(8,128)} %all-gather.11.cloned.1.call-done), kind=kOutput, calls=%fused_computation.36 | convolution fusion | flops 6442450944 | bytes 17039360 | tf_op jit(solution)/shard_map/dot_general | solution.py:14
  478.5 7.8 %all-gather.3 = f32[512,256]{0,1:T(8,128)S(1)} all-gather(f32[256,256]{0,1:T(8,128)S(1)} %fusion.20), channel_id=5, replica_groups=mesh['row'=2,'col'=16] {'row'}, dimensions={0}, use_global_device_ids=true | all-gather | bytes 786432 | tf_op jit(solution)/shard_map/all_gather | solution.py:33
  487.3 1.3 fusion.27
  488.6 11.9 %fusion.4 = f32[8192,256]{0,1:T(8,128)S(1)} fusion(f32[8192,256]{0,1:T(8,128)} %copy-done.3, f32[256,256]{1,0:T(8,128)S(1)} %fusion.27, f32[8,8192,256]{1,2,0:T(8,128)} %all-gather.11.cloned.1.call-done), kind=kOutput, calls=%fused_computation.9 | convolution fusion | flops 6444548096 | bytes 25427968 | tf_op jit(solution)/shard_map/dot_general | solution.py:10
  500.5 12.5 %fusion.19 = f32[256,256]{0,1:T(8,128)S(1)} fusion(f32[8192,256]{0,1:T(8,128)S(1)} %fusion.4, f32[8,8192,256]{1,2,0:T(8,128)} %all-gather.11.cloned.1.call-done), kind=kOutput, calls=%fused_computation.35 | convolution fusion | flops 6442450944 | bytes 17039360 | tf_op jit(solution)/shard_map/dot_general | solution.py:14
  513.0 7.2 %all-gather.4 = f32[512,256]{0,1:T(8,128)S(1)} all-gather(f32[256,256]{0,1:T(8,128)S(1)} %fusion.19), channel_id=6, replica_groups=mesh['row'=2,'col'=16] {'row'}, dimensions={0}, use_global_device_ids=true | all-gather | bytes 786432 | tf_op jit(solution)/shard_map/all_gather | solution.py:33
  521.2 1.3 fusion.26
  522.5 11.9 %fusion.3 = f32[8192,256]{0,1:T(8,128)S(1)} fusion(f32[8192,256]{0,1:T(8,128)} %copy-done.4, f32[256,256]{1,0:T(8,128)S(1)} %fusion.26, f32[8,8192,256]{1,2,0:T(8,128)} %all-gather.11.cloned.1.call-done), kind=kOutput, calls=%fused_computation.7 | convolution fusion | flops 6444548096 | bytes 25427968 | tf_op jit(solution)/shard_map/dot_general | solution.py:10
  534.5 12.5 %fusion.18 = f32[256,256]{0,1:T(8,128)S(1)} fusion(f32[8192,256]{0,1:T(8,128)S(1)} %fusion.3, f32[8,8192,256]{1,2,0:T(8,128)} %all-gather.11.cloned.1.call-done), kind=kOutput, calls=%fused_computation.34 | convolution fusion | flops 6442450944 | bytes 17039360 | tf_op jit(solution)/shard_map/dot_general | solution.py:14
  546.9 7.3 %all-gather.5 = f32[512,256]{0,1:T(8,128)S(1)} all-gather(f32[256,256]{0,1:T(8,128)S(1)} %fusion.18), channel_id=7, replica_groups=mesh['row'=2,'col'=16] {'row'}, dimensions={0}, use_global_device_ids=true | all-gather | bytes 786432 | tf_op jit(solution)/shard_map/all_gather | solution.py:33
  555.2 1.3 fusion.25
  556.5 11.9 %fusion.2 = f32[8192,256]{0,1:T(8,128)S(1)} fusion(f32[8192,256]{0,1:T(8,128)} %copy-done.5, f32[256,256]{1,0:T(8,128)S(1)} %fusion.25, f32[8,8192,256]{1,2,0:T(8,128)} %all-gather.11.cloned.1.call-done), kind=kOutput, calls=%fused_computation.5 | convolution fusion | flops 6444548096 | bytes 25427968 | tf_op jit(solution)/shard_map/dot_general | solution.py:10
  568.4 12.5 %fusion.17 = f32[256,256]{0,1:T(8,128)S(1)} fusion(f32[8192,256]{0,1:T(8,128)S(1)} %fusion.2, f32[8,8192,256]{1,2,0:T(8,128)} %all-gather.11.cloned.1.call-done), kind=kOutput, calls=%fused_computation.33 | convolution fusion | flops 6442450944 | bytes 17039360 | tf_op jit(solution)/shard_map/dot_general | solution.py:14
  580.9 7.3 %all-gather.6 = f32[512,256]{0,1:T(8,128)S(1)} all-gather(f32[256,256]{0,1:T(8,128)S(1)} %fusion.17), channel_id=8, replica_groups=mesh['row'=2,'col'=16] {'row'}, dimensions={0}, use_global_device_ids=true | all-gather | bytes 786432 | tf_op jit(solution)/shard_map/all_gather | solution.py:33
  590.5 11.9 %fusion.1 = f32[8192,256]{0,1:T(8,128)S(1)} fusion(f32[8192,256]{0,1:T(8,128)} %copy-done.6, f32[256,256]{1,0:T(8,128)S(1)} %fusion.24, f32[8,8192,256]{1,2,0:T(8,128)} %all-gather.11.cloned.1.call-done), kind=kOutput, calls=%fused_computation.3 | convolution fusion | flops 6444548096 | bytes 25427968 | tf_op jit(solution)/shard_map/dot_general | solution.py:10
  602.4 12.5 %fusion.16 = f32[256,256]{0,1:T(8,128)S(1)} fusion(f32[8192,256]{0,1:T(8,128)S(1)} %fusion.1, f32[8,8192,256]{1,2,0:T(8,128)} %all-gather.11.cloned.1.call-done), kind=kOutput, calls=%fused_computation.32 | convolution fusion | flops 6442450944 | bytes 17039360 | tf_op jit(solution)/shard_map/dot_general | solution.py:14
  614.9 7.3 %all-gather.7 = f32[512,256]{0,1:T(8,128)S(1)} all-gather(f32[256,256]{0,1:T(8,128)S(1)} %fusion.16), channel_id=9, replica_groups=mesh['row'=2,'col'=16] {'row'}, dimensions={0}, use_global_device_ids=true | all-gather | bytes 786432 | tf_op jit(solution)/shard_map/all_gather | solution.py:33
  624.5 16.2 %fusion = f32[8192,256]{0,1:T(8,128)} fusion(f32[8192,256]{0,1:T(8,128)} %copy-done, f32[256,256]{1,0:T(8,128)S(1)} %fusion.23, f32[8,8192,256]{1,2,0:T(8,128)} %all-gather.11.cloned.1.call-done), kind=kOutput, calls=%fused_computation.1 | convolution fusion | flops 6444548096 | bytes 25427968 | tf_op jit(solution)/shard_map/dot_general | solution.py:10
  640.7 9.0 %copy.7 = f32[8192,256]{1,0:T(8,128)} copy(f32[8192,256]{0,1:T(8,128)} %fusion) | data formatting | bytes 16777216 | tf_op jit(solution)/shard_map/sub | solution.py:34
  (37 shorter events, 13.5 us)
Async XLA Ops:
  6.5 331.2 %all-gather.11.cloned.1.call-start = ((), (), s32[]{:S(2)}) async-start(), calls=%async_computation | async-start | bytes 71303168 | tf_op jit(solution)/shard_map/all_gather | solution.py:26
  7.3 374.2 %all-gather.13.cloned.1.call-start = ((), (), s32[]{:S(2)}) async-start(), calls=%async_computation.1 | async-start | bytes 2228224 | tf_op jit(solution)/shard_map/all_gather | solution.py:27
  394.9 12.5 %copy-start.1 = (f32[8192,256]{0,1:T(8,128)}, f32[8192,256]{0,1:T(8,128)S(1)}, u32[]{:S(2)}) copy-start(f32[8192,256]{0,1:T(8,128)S(1)} %fusion.7) | copy-start | bytes 25165828
  430.9 12.5 %copy-start.2 = (f32[8192,256]{0,1:T(8,128)}, f32[8192,256]{0,1:T(8,128)S(1)}, u32[]{:S(2)}) copy-start(f32[8192,256]{0,1:T(8,128)S(1)} %fusion.6) | copy-start | bytes 25165828
  466.0 12.5 %copy-start.3 = (f32[8192,256]{0,1:T(8,128)}, f32[8192,256]{0,1:T(8,128)S(1)}, u32[]{:S(2)}) copy-start(f32[8192,256]{0,1:T(8,128)S(1)} %fusion.5) | copy-start | bytes 25165828
  500.5 12.5 %copy-start.4 = (f32[8192,256]{0,1:T(8,128)}, f32[8192,256]{0,1:T(8,128)S(1)}, u32[]{:S(2)}) copy-start(f32[8192,256]{0,1:T(8,128)S(1)} %fusion.4) | copy-start | bytes 25165828
  534.4 12.5 %copy-start.5 = (f32[8192,256]{0,1:T(8,128)}, f32[8192,256]{0,1:T(8,128)S(1)}, u32[]{:S(2)}) copy-start(f32[8192,256]{0,1:T(8,128)S(1)} %fusion.3) | copy-start | bytes 25165828
  568.4 12.5 %copy-start.6 = (f32[8192,256]{0,1:T(8,128)}, f32[8192,256]{0,1:T(8,128)S(1)}, u32[]{:S(2)}) copy-start(f32[8192,256]{0,1:T(8,128)S(1)} %fusion.2) | copy-start | bytes 25165828
  602.4 12.5 %copy-start = (f32[8192,256]{0,1:T(8,128)}, f32[8192,256]{0,1:T(8,128)S(1)}, u32[]{:S(2)}) copy-start(f32[8192,256]{0,1:T(8,128)S(1)} %fusion.1) | copy-start | bytes 25165828
Sparse Core Ops, SparseCore 0:
  8.9 328.7 all-gather.10
  339.9 41.4 all-gather.12
